TPU v7x, 32 devices: a whole 2x2x4 slice. The times are simulated.
32 devices in a mesh: freq: 2 (over core), row: 4 (over y, x), col: 4 (over z).
Axes of the slice: x: 2, y: 2, z: 4, core: 2. Of those that a mesh axis runs over, the one named last changes fastest.
Arguments:
- coupling: bfloat16 [6144, 6144], P('row', 'col'), may hold values from -0.15625 to 0.15625
- freq_weight: float32 [12288], P(('freq', 'row')), parts along dimension 0, may hold values from 0.05 to 2
Outputs:
- response: float32 [12288, 6144], P(('freq', 'row'), 'col'), parts along dimension 0
There are 2 independent parts, one for each index of `freq`. A program takes and returns all parts, laid end to end along the dimension named above; an argument that names none is the same for every part. Nothing has to cross between parts.
All inputs are finite; a program needn't handle non-finite values.
Results may differ from a plain program's by a relative error of at most 0.0021.
Values may be sent and summed in bfloat16 or wider, within the bound.
A program may use at most 128 MiB of HBM per device.

v0:
```python
import jax
import jax.numpy as jnp
from jax import lax
from jax.sharding import PartitionSpec as P


def on_device(coupling, freq_weight):
    weighted = (coupling.astype(jnp.float32) * freq_weight[:, None]).astype(jnp.bfloat16)
    full_rows = lax.all_gather(weighted, "col", axis=1, tiled=True)
    return lax.psum_scatter(
        lax.dot_general(
            full_rows, coupling, (((0,), (0,)), ((), ())), preferred_element_type=jnp.float32
        ),
        "row",
        scatter_dimension=0,
        tiled=True,
    )


def solution(mesh):
    placed = (P("row", "col"), P(("freq", "row")))
    return jax.shard_map(
        on_device, mesh=mesh, in_specs=placed, out_specs=P(("freq", "row"), "col"), check_vma=False
    )
```

profile of v0, /device:TPU:0, one launch (start us, length us, event | category | flops | bytes accessed | tf_op | source)
XLA Modules:
  0.0 702.4 jit_solution(10874687154043378415)
XLA Ops:
  6.5 0.0 all-gather.2.cloned.1.call-start
  6.5 5.4 multiply_convert_fusion
  11.9 0.0 all-gather.2.cloned.1.call-update
  11.9 0.0 reduce-scatter.2.cloned.1.call-start
  12.0 325.4 %all-gather.2.cloned.1.call-done = bf16[1536,6144]{1,0:T(8,128)(2,1)} async-done(((bf16[1536,1536]{1,0:T(8,128)(2,1)}), bf16[1536,6144]{1,0:T(8,128)(2,1)}) %all-gather.2.cloned.1.call-update) | async-done | bytes 18874384 | tf_op jit(solution)/shard_map/all_gather | solution.py:9
  337.4 36.7 %fusion = f32[6144,1536]{1,0:T(8,128)} fusion(bf16[1536,6144]{1,0:T(8,128)(2,1)} %all-gather.2.cloned.1.call-done, bf16[1536,1536]{1,0:T(8,128)(2,1)} %param.2), kind=kOutput, calls=%fused_computation.1 | convolution fusion | flops 28991029248 | bytes 61341696 | tf_op jit(solution)/shard_map/dot_general | solution.py:11
  374.1 0.0 reduce-scatter.2.cloned.1.call-update
  374.1 321.4 %reduce-scatter.2.cloned.1.call-done = f32[1536,1536]{1,0:T(8,128)} async-done(((f32[6144,1536]{1,0:T(8,128)}), f32[1536,1536]{1,0:T(8,128)}) %reduce-scatter.2.cloned.1.call-update) | async-done | bytes 9437200 | tf_op jit(solution)/shard_map/reduce_scatter | solution.py:10
Async XLA Ops:
  6.5 330.8 %all-gather.2.cloned.1.call-start = ((), (), s32[]{:S(2)}) async-start(), calls=%async_computation.1 | async-start | bytes 23592960 | tf_op jit(solution)/shard_map/all_gather | solution.py:9
  11.9 683.6 %reduce-scatter.2.cloned.1.call-start = ((), (), s32[]{:S(2)}) async-start(), calls=%async_computation.2 | async-start | bytes 47185920 | tf_op jit(solution)/shard_map/reduce_scatter | solution.py:10
Sparse Core Ops, SparseCore 0:
  12.0 325.2 all-gather.1
  374.2 321.2 reduce-scatter.1
where the time goes:
time: 703 us; the launch traced here: 702 us
  waiting for transfers between devices  647 us (92%)
  matrix products  36.7 us (5%)
  between operations  13.4 us (2%)
    all_gather x1, waiting for transfers between devices, on_device(): full_rows = lax.all_gather(weighted, 'col', axis=1, tiled=True)  325 us
    reduce_scatter x1, waiting for transfers between devices, on_device(): lax.psum_scatter(lax.dot_general(full_rows, coupling, (((0,), (0,)), ((),...  321 us
    dot_general x1, matrix products, on_device(): lax.dot_general(full_rows, coupling, (((0,), (0,)), ((), ())), preferred_...  36.7 us
  transfers between devices with their start and end apart: 2, of which 2 were waited for; matrix products, arithmetic and copies ran while one was open for 0% of the time, Pallas kernels for 0%

commit v1 on v0

--- a/solution.py
+++ b/solution.py
@@ -4,9 +4,19 @@
 from jax.sharding import PartitionSpec as P
 
 
+def pass_along(x, axis, d):
+    count = lax.axis_size(axis)
+    held, shards = (x, [x])
+    for _ in range(count - 1):
+        held = lax.ppermute(held, axis, [(i, (i + 1) % count) for i in range(count)])
+        shards.insert(0, held)
+    row_of_blocks = jnp.concatenate(shards, axis=d)
+    return jnp.roll(row_of_blocks, (lax.axis_index(axis) + 1) * x.shape[d], axis=d)
+
+
 def on_device(coupling, freq_weight):
     weighted = (coupling.astype(jnp.float32) * freq_weight[:, None]).astype(jnp.bfloat16)
-    full_rows = lax.all_gather(weighted, "col", axis=1, tiled=True)
+    full_rows = pass_along(weighted, "col", 1)
     return lax.psum_scatter(
         lax.dot_general(
             full_rows, coupling, (((0,), (0,)), ((), ())), preferred_element_type=jnp.float32

time: 703 us -> 723 us (1.028)
  local copies, waits for them, and re-layouts: 0 us -> 26.7 us
  waiting for transfers between devices: 647 us -> 633 us
    all_gather x1 -> x0, waiting for transfers between devices: 325 us -> none  [on_device(): full_rows = lax.all_gather(weighted, 'col', axis=1, tiled=True)]
    ppermute x0 -> x3, waiting for transfers between devices: none -> 313 us  [pass_along(): lax.ppermute(held, axis, [(i, (i + 1) % count) for i in range(count)])]
    unnamed x0 -> x18, local copies, waits for them, and re-layouts: none -> 26.7 us
  transfers between devices with their start and end apart: 2 -> 4, of which waited for: 2 -> 4; matrix products, arithmetic and copies ran while one was open for 0% -> 0% of each run, Pallas kernels for 0% -> 0%
where the time goes in v1:
time: 723 us
  waiting for transfers between devices  633 us (88%)
  matrix products  37 us (5%)
  local copies, waits for them, and re-layouts  26.7 us (4%)
  between operations  13.4 us (2%)
  other arithmetic  9.41 us (1%)
    reduce_scatter x1, waiting for transfers between devices, on_device(): lax.psum_scatter(lax.dot_general(full_rows, coupling, (((0,), (0,)), ((),...  320 us
    ppermute x3, waiting for transfers between devices, pass_along(): lax.ppermute(held, axis, [(i, (i + 1) % count) for i in range(count)])  313 us
    dot_general x1, matrix products, on_device(): lax.dot_general(full_rows, coupling, (((0,), (0,)), ((), ())), preferred_...  37 us
    unnamed x18, local copies, waits for them, and re-layouts  26.7 us
  transfers between devices with their start and end apart: 4, of which 4 were waited for; matrix products, arithmetic and copies ran while one was open for 0% of the time, Pallas kernels for 0%

profile of v1, /device:TPU:0, one launch (start us, length us, event | category | flops | bytes accessed | tf_op | source)
XLA Modules:
  0.0 722.9 jit_solution(16285318171752467127)
XLA Ops:
  6.5 0.0 slice-start
  6.5 0.0 copy-start.1
  6.5 0.0 reduce-scatter.2.cloned.1.call-start
  6.5 3.2 multiply_convert_fusion
  9.8 3.1 collective-permute-start
  12.9 103.8 %collective-permute-done = bf16[1536,1536]{1,0:T(8,128)(2,1)S(1)} collective-permute-done((bf16[1536,1536]{1,0:T(8,128)(2,1)S(1)}, bf16[1536,1536]{1,0:T(8,128)(2,1)S(1)}, u32[]{:S(2)}, u32[]{:S(2)}) %collective-permute-start) | collective-permute-done | bytes 4718624 | tf_op jit(solution)/shard_map/ppermute | solution.py:11
  116.7 0.0 copy-start
  116.7 2.2 copy-done
  118.9 0.0 collective-permute-start.1
  118.9 104.9 %collective-permute-done.1 = bf16[1536,1536]{1,0:T(8,128)(2,1)} collective-permute-done((bf16[1536,1536]{1,0:T(8,128)(2,1)S(1)}, bf16[1536,1536]{1,0:T(8,128)(2,1)}, u32[]{:S(2)}, u32[]{:S(2)}) %collective-permute-start.1) | collective-permute-done | bytes 4718624 | tf_op jit(solution)/shard_map/ppermute | solution.py:11
  223.8 0.0 collective-permute-start.2
  223.8 0.0 slice-start.2
  223.8 0.0 slice-start.1
  223.8 104.2 %collective-permute-done.2 = bf16[1536,1536]{1,0:T(8,128)(2,1)} collective-permute-done((bf16[1536,1536]{1,0:T(8,128)(2,1)}, bf16[1536,1536]{1,0:T(8,128)(2,1)}, u32[]{:S(2)}, u32[]{:S(2)}) %collective-permute-start.2) | collective-permute-done | bytes 4718624 | tf_op jit(solution)/shard_map/ppermute | solution.py:11
  328.0 4.8 constant_dynamic-update-slice_fusion.7
  332.9 0.0 slice-start.3
  332.9 5.0 constant_dynamic-update-slice_fusion.6
  337.8 0.0 slice-done.2
  337.8 0.0 slice-done.3
  337.8 2.5 constant_dynamic-update-slice_fusion.5
  340.4 0.0 slice-done
  340.4 0.0 copy-done.1
  340.4 0.0 slice-done.1
  340.4 3.0 constant_dynamic-update-slice_fusion.4
  343.4 4.8 constant_dynamic-update-slice_fusion.3
  348.2 4.8 constant_dynamic-update-slice_fusion.2
  353.1 2.5 constant_dynamic-update-slice_fusion.1
  355.6 3.1 constant_dynamic-update-slice_fusion
  358.7 37.0 %fusion = f32[6144,1536]{1,0:T(8,128)} fusion(bf16[1536,1536]{1,0:T(8,128)(2,1)S(1)} %bitcast.2, bf16[1536,12288]{1,0:T(8,128)(2,1)} %constant_dynamic-update-slice_fusion, s32[]{:T(128)S(6)} %select_n.14), kind=kOutput, calls=%fused_computation | convolution fusion | flops 28991029248 | bytes 61341700 | tf_op jit(solution)/shard_map/dot_general | solution.py:21
  395.7 0.0 reduce-scatter.2.cloned.1.call-update
  395.8 320.3 %reduce-scatter.2.cloned.1.call-done = f32[1536,1536]{1,0:T(8,128)} async-done(((f32[6144,1536]{1,0:T(8,128)}), f32[1536,1536]{1,0:T(8,128)}) %reduce-scatter.2.cloned.1.call-update) | async-done | bytes 9437200 | tf_op jit(solution)/shard_map/reduce_scatter | solution.py:20
  (2 shorter events, 0.0 us)
Async XLA Ops:
  6.5 333.8 %slice-start = ((s8[4718592]{0:T(1024)(128)(4,1)}), s8[524288]{0:T(1024)(128)(4,1)S(1)}, s32[]{:S(2)}) async-start(s8[4718592]{0:T(1024)(128)(4,1)} %bitcast.1), calls=%async_computation.2 | async-start | bytes 1048576
  6.5 333.8 %copy-start.1 = (f32[1536]{0:T(1024)S(1)}, f32[1536]{0:T(1024)}, u32[]{:S(2)}) copy-start(f32[1536]{0:T(1024)} %param.3) | copy-start | bytes 18436
  6.5 709.5 %reduce-scatter.2.cloned.1.call-start = ((), (), s32[]{:S(2)}) async-start(), calls=%async_computation.1 | async-start | bytes 47185920 | tf_op jit(solution)/shard_map/reduce_scatter | solution.py:20
  9.8 106.9 %collective-permute-start = (bf16[1536,1536]{1,0:T(8,128)(2,1)S(1)}, bf16[1536,1536]{1,0:T(8,128)(2,1)S(1)}, u32[]{:S(2)}, u32[]{:S(2)}) collective-permute-start(bf16[1536,1536]{1,0:T(8,128)(2,1)S(1)} %multiply_convert_fusion), channel_id=1, source_target_pairs={{0,1},{1,2},{2,3},{3,0},{4,5},{5,6},{6,7},{7,4},{8,9},{9,10},{10,1... | collective-permute-start | bytes 14155784 | tf_op jit(solution)/shard_map/ppermute | solution.py:11
  116.7 2.2 copy-start
  118.9 104.9 %collective-permute-start.1 = (bf16[1536,1536]{1,0:T(8,128)(2,1)S(1)}, bf16[1536,1536]{1,0:T(8,128)(2,1)}, u32[]{:S(2)}, u32[]{:S(2)}) collective-permute-start(bf16[1536,1536]{1,0:T(8,128)(2,1)S(1)} %collective-permute-done), channel_id=1, source_target_pairs={{0,1},{1,2},{2,3},{3,0},{4,5},{5,6},{6,7},{7,4},{8,9},{9,10},{10,1... | collective-permute-start | bytes 14155784 | tf_op jit(solution)/shard_map/ppermute | solution.py:11
  223.8 104.2 %collective-permute-start.2 = (bf16[1536,1536]{1,0:T(8,128)(2,1)}, bf16[1536,1536]{1,0:T(8,128)(2,1)}, u32[]{:S(2)}, u32[]{:S(2)}) collective-permute-start(bf16[1536,1536]{1,0:T(8,128)(2,1)} %collective-permute-done.1), channel_id=1, source_target_pairs={{0,1},{1,2},{2,3},{3,0},{4,5},{5,6},{6,7},{7,4},{8,9},{9,10},{10,1... | collective-permute-start | bytes 14155784 | tf_op jit(solution)/shard_map/ppermute | solution.py:11
  223.8 114.0 %slice-start.2 = ((s8[4718592]{0:T(1024)(128)(4,1)}), s8[4194304]{0:T(1024)(128)(4,1)S(1)}, s32[]{:S(2)}) async-start(s8[4718592]{0:T(1024)(128)(4,1)} %bitcast.3), calls=%async_computation.4 | async-start | bytes 8388608
  223.8 116.6 %slice-start.1 = ((s8[4718592]{0:T(1024)(128)(4,1)}), s8[4194304]{0:T(1024)(128)(4,1)S(1)}, s32[]{:S(2)}) async-start(s8[4718592]{0:T(1024)(128)(4,1)} %bitcast.1), calls=%async_computation.3 | async-start | bytes 8388608
  332.9 5.0 slice-start.3
Sparse Core Ops, SparseCore 0:
  395.9 320.1 reduce-scatter.1
